TPU v7x, 32 devices: a whole 2x2x4 slice. The times are simulated.
32 devices in a mesh: dp: 4 (over z), tensor: 8 (over y, x, core).
Axes of the slice: x: 2, y: 2, z: 4, core: 2. Of those that a mesh axis runs over, the one named last changes fastest.
Arguments:
- tokens: bfloat16 [1024, 4096], P(('dp', 'tensor')), may hold values from -4 to 4
- lengths: int32 [4], replicated, may hold values from 64 to 256, as said below
- norm_gains: float32 [2, 4096], replicated, may hold values from 0.25 to 1.75
- query_weight: bfloat16 [2, 4096, 4096], P(None, None, 'tensor'), may hold values from -0.09375 to 0.09375
- key_weight: bfloat16 [2, 4096, 1024], P(None, None, 'tensor'), may hold values from -0.09375 to 0.09375
- value_weight: bfloat16 [2, 4096, 1024], P(None, None, 'tensor'), may hold values from -0.09375 to 0.09375
- out_weight: bfloat16 [2, 4096, 4096], P(None, 'tensor'), may hold values from -0.09375 to 0.09375
- query_probe: bfloat16 [2, 4096, 4096], P(None, 'dp', 'tensor'), may hold values from -0.09375 to 0.09375
- key_probe: bfloat16 [2, 4096, 1024], P(None, 'dp', 'tensor'), may hold values from -0.09375 to 0.09375
- value_probe: bfloat16 [2, 4096, 1024], P(None, 'dp', 'tensor'), may hold values from -0.09375 to 0.09375
- out_probe: bfloat16 [2, 4096, 4096], P(None, 'tensor', 'dp'), may hold values from -0.09375 to 0.09375
Outputs:
- query_product: float32 [2, 4096, 4096], P(None, 'dp', 'tensor')
- key_product: float32 [2, 4096, 1024], P(None, 'dp', 'tensor')
- value_product: float32 [2, 4096, 1024], P(None, 'dp', 'tensor')
- out_product: float32 [2, 4096, 4096], P(None, 'tensor', 'dp')
Inputs may be any that keep to these rules, and one draw needn't show every extreme that they name: lengths[i] counts the leading valid positions of sequence i; the last sequence is full.
All inputs are finite; a program needn't handle non-finite values.
Results may differ from a plain program's by a relative error of at most 0.035.
Values may be sent and summed in bfloat16 or wider, within the bound.
A program may use at most 128 MiB of HBM per device.

v0:
```python
import math
import jax
import jax.numpy as jnp
from jax import lax
from jax.sharding import PartitionSpec as P

KVH = 8
HD = 128
LEN = 256
EPS = 1e-05
THETA = 500000.0


def swapped(value, axis, apart):
    mask = 2**apart
    pairs = [(source, source ^ mask) for source in range(lax.axis_size(axis))]
    return lax.ppermute(value, axis, pairs)


def multiply(pattern, left_side, right_side):
    return jnp.einsum(pattern, left_side, right_side, preferred_element_type=jnp.float32)


def matmul(left_side, right_side):
    return jnp.dot(left_side, right_side, preferred_element_type=jnp.float32)


def contract_rows(left_side, right_side):
    return lax.dot_general(
        left_side, right_side, (((0,), (0,)), ((), ())), preferred_element_type=jnp.float32
    )


def contract_last(left_side, right_side):
    return lax.dot_general(
        left_side, right_side, (((1,), (1,)), ((), ())), preferred_element_type=jnp.float32
    )


def rope_tables(length, head_size):
    position = jnp.arange(length).astype(jnp.float32)
    column = jnp.arange(head_size // 2).astype(jnp.float32)
    frequency = jnp.exp(-math.log(THETA) * 2.0 * column / head_size)
    angles = position[:, None] * frequency[None, :]
    return (jnp.cos(angles), jnp.sin(angles))


def rotate(values, cosine_table, sine_table, direction):
    middle = values.shape[-1] // 2
    leading = values[..., :middle]
    trailing = values[..., middle:]
    cosine = cosine_table[None, :, None, :]
    sine_part = direction * sine_table[None, :, None, :]
    return jnp.concatenate(
        [leading * cosine - trailing * sine_part, trailing * cosine + leading * sine_part], axis=-1
    )


def allowed_mask(size, length):
    row_index = jnp.arange(size)[:, None]
    column_index = jnp.arange(size)[None, :]
    return (column_index <= row_index) & (column_index < length)


def attend(queries, key_heads, value_heads, tangent_queries, tangent_keys, tangent_values, length):
    repeat = queries.shape[1] // key_heads.shape[1]
    key_heads = jnp.repeat(key_heads, repeat, axis=1)
    value_heads = jnp.repeat(value_heads, repeat, axis=1)
    tangent_keys = jnp.repeat(tangent_keys, repeat, axis=1)
    tangent_values = jnp.repeat(tangent_values, repeat, axis=1)
    scaling = 1.0 / math.sqrt(queries.shape[-1])
    allowed = allowed_mask(queries.shape[0], length)[None]
    scores = multiply("ihd,jhd->hij", queries, key_heads) * scaling
    powers = jnp.where(allowed, jnp.exp(scores), 0.0)
    weights = powers / jnp.sum(powers, axis=-1, keepdims=True)
    weights_low = weights.astype(jnp.bfloat16)
    blended = multiply("hij,jhd->ihd", weights_low, value_heads).astype(jnp.bfloat16)
    tangent_scores = (
        multiply("ihd,jhd->hij", tangent_queries, key_heads)
        + multiply("ihd,jhd->hij", queries, tangent_keys)
    ) * scaling
    tangent_weights = weights * (
        tangent_scores - jnp.sum(weights * tangent_scores, axis=-1, keepdims=True)
    )
    tangent_blended = multiply(
        "hij,jhd->ihd", tangent_weights.astype(jnp.bfloat16), value_heads
    ) + multiply("hij,jhd->ihd", weights_low, tangent_values)
    return (blended, tangent_blended.astype(jnp.bfloat16))


def attend_back(queries, key_heads, value_heads, grad_mixed, length):
    repeat = queries.shape[1] // key_heads.shape[1]
    key_heads = jnp.repeat(key_heads, repeat, axis=1)
    value_heads = jnp.repeat(value_heads, repeat, axis=1)
    scaling = 1.0 / math.sqrt(queries.shape[-1])
    allowed = allowed_mask(queries.shape[0], length)[None]
    scores = multiply("ihd,jhd->hij", queries, key_heads) * scaling
    powers = jnp.where(allowed, jnp.exp(scores), 0.0)
    weights = powers / jnp.sum(powers, axis=-1, keepdims=True)
    weights_low = weights.astype(jnp.bfloat16)
    grad_weights = multiply("ihd,jhd->hij", grad_mixed, value_heads)
    grad_values = multiply("hij,ihd->jhd", weights_low, grad_mixed)
    grad_scores = (
        weights * (grad_weights - jnp.sum(weights * grad_weights, axis=-1, keepdims=True)) * scaling
    ).astype(jnp.bfloat16)
    grad_queries = multiply("hij,jhd->ihd", grad_scores, key_heads)
    grad_keys = multiply("hij,ihd->jhd", grad_scores, queries)
    return (grad_queries, grad_keys, grad_values)


def normalize(stream, gain_row):
    wide_stream = stream.astype(jnp.float32)
    inverse = lax.rsqrt(jnp.mean(wide_stream * wide_stream, axis=-1, keepdims=True) + EPS)
    return (wide_stream, inverse, (wide_stream * inverse * gain_row).astype(jnp.bfloat16))


def norm_tangent(wide_stream, inverse, tangent, gain_row):
    shift = jnp.mean(wide_stream * tangent, axis=-1, keepdims=True)
    return (
        gain_row * (tangent * inverse - wide_stream * inverse * inverse * inverse * shift)
    ).astype(jnp.bfloat16)


def norm_back(wide_stream, inverse, grad_normed, gain_row):
    scaled = grad_normed * gain_row
    shift = jnp.mean(wide_stream * scaled, axis=-1, keepdims=True)
    return inverse * (scaled - wide_stream * inverse * inverse * shift)


def body(
    tokens,
    lengths,
    norm_gains,
    query_weight,
    key_weight,
    value_weight,
    out_weight,
    query_probe,
    key_probe,
    value_probe,
    out_probe,
):
    tensor_count = lax.axis_size("tensor")
    tensor_index = lax.axis_index("tensor")
    data_index = lax.axis_index("dp")
    share_rows = tokens.shape[0]
    group_rows = share_rows * tensor_count
    seq_count = group_rows // LEN
    layer_count = query_weight.shape[0]
    half_width = key_weight.shape[2]
    cosine_table, sine_table = rope_tables(LEN, HD)
    group_lengths = lax.dynamic_slice_in_dim(lengths, data_index * seq_count, seq_count)
    position = jnp.arange(group_rows) % LEN
    group_mask = (position < jnp.repeat(group_lengths, LEN)).astype(jnp.float32)
    lower_half = tensor_index % 2 == 0
    paired = tensor_count > KVH

    def heads_of(values):
        return values.reshape(seq_count, LEN, -1, HD)

    def join_halves(own_part, other_part):
        return jnp.where(
            lower_half,
            jnp.concatenate([own_part, other_part], axis=-1),
            jnp.concatenate([other_part, own_part], axis=-1),
        )

    def own_columns(values):
        return jnp.where(lower_half, values[:, :half_width], values[:, half_width:])

    def other_columns(values):
        return jnp.where(lower_half, values[:, half_width:], values[:, :half_width])

    query_full_probe, key_own_probe, value_own_probe, out_full_probe = (
        lax.all_gather(query_probe, "dp", axis=1, tiled=True),
        lax.all_gather(key_probe, "dp", axis=1, tiled=True),
        lax.all_gather(value_probe, "dp", axis=1, tiled=True),
        lax.all_gather(out_probe, "dp", axis=2, tiled=True),
    )
    owned_parts = (key_weight, value_weight, key_own_probe, value_own_probe)
    if paired:
        partner = swapped((key_weight, value_weight, key_own_probe, value_own_probe), "tensor", 0)
        joined = [
            join_halves(own_part, other_part) for own_part, other_part in zip(owned_parts, partner)
        ]
        key_full, value_full, key_full_probe, value_full_probe = joined
    else:
        key_full, value_full, key_full_probe, value_full_probe = owned_parts
    stream = lax.all_gather(tokens, "tensor", axis=0, tiled=True)
    tangent = None
    stored = []
    for layer_index in range(layer_count):
        final_layer = layer_index == layer_count - 1
        gain_row = norm_gains[layer_index]
        wide_stream, inverse, normed = normalize(stream, gain_row)
        tangent_normed = (
            None if tangent is None else norm_tangent(wide_stream, inverse, tangent, gain_row)
        )
        normed_all, tangent_all = (normed, tangent_normed)

        def project(weight, probe_part):
            primal = matmul(normed_all, weight)
            moved_part = matmul(normed_all, probe_part)
            if tangent_all is not None:
                moved_part = moved_part + matmul(tangent_all, weight)
            return (primal, moved_part)

        query_primal, query_moved = project(
            query_weight[layer_index], query_full_probe[layer_index]
        )
        key_primal, key_moved = project(key_full[layer_index], key_full_probe[layer_index])
        value_primal, value_moved = project(value_full[layer_index], value_full_probe[layer_index])
        queries = rotate(heads_of(query_primal), cosine_table, sine_table, 1.0).astype(jnp.bfloat16)
        key_heads = rotate(heads_of(key_primal), cosine_table, sine_table, 1.0).astype(jnp.bfloat16)
        value_heads = heads_of(value_primal).astype(jnp.bfloat16)
        tangent_queries = rotate(heads_of(query_moved), cosine_table, sine_table, 1.0).astype(
            jnp.bfloat16
        )
        tangent_keys = rotate(heads_of(key_moved), cosine_table, sine_table, 1.0).astype(
            jnp.bfloat16
        )
        tangent_values = heads_of(value_moved).astype(jnp.bfloat16)
        blended, tangent_blended = lax.map(
            lambda pieces: attend(*pieces),
            (
                queries,
                key_heads,
                value_heads,
                tangent_queries,
                tangent_keys,
                tangent_values,
                group_lengths,
            ),
        )
        blended = blended.reshape(group_rows, -1)
        tangent_blended = tangent_blended.reshape(group_rows, -1)
        tangent_part = matmul(tangent_blended, out_weight[layer_index]) + matmul(
            blended, out_full_probe[layer_index]
        )
        if final_layer:
            tangent_sum = lax.psum(tangent_part.astype(jnp.bfloat16), "tensor").astype(jnp.float32)
        else:
            primal_part = matmul(blended, out_weight[layer_index])
            primal_sum, tangent_sum = (
                lax.psum(primal_part.astype(jnp.bfloat16), "tensor").astype(jnp.float32),
                lax.psum(tangent_part.astype(jnp.bfloat16), "tensor").astype(jnp.float32),
            )
        stored.append((wide_stream, inverse, normed_all, queries, key_heads, value_heads, blended))
        if not final_layer:
            stream = (wide_stream + primal_sum).astype(jnp.bfloat16)
        tangent = tangent_sum if tangent is None else tangent + tangent_sum
    cotangent = group_mask[:, None] * tangent
    collected = [None] * layer_count
    for layer_index in reversed(range(layer_count)):
        wide_stream, inverse, normed_all, queries, key_heads, value_heads, blended = stored[
            layer_index
        ]
        cotangent_low = cotangent.astype(jnp.bfloat16)
        out_product = contract_rows(blended, cotangent_low)
        grad_mixed = contract_last(cotangent_low, out_weight[layer_index]).astype(jnp.bfloat16)
        grad_queries, grad_keys, grad_values = lax.map(
            lambda pieces: attend_back(*pieces),
            (queries, key_heads, value_heads, heads_of(grad_mixed), group_lengths),
        )
        key_count = key_heads.shape[2]
        query_low = (
            rotate(grad_queries, cosine_table, sine_table, -1.0)
            .astype(jnp.bfloat16)
            .reshape(group_rows, -1)
        )
        key_grouped = grad_keys.reshape(seq_count, LEN, key_count, -1, HD).sum(axis=3)
        key_low = (
            rotate(key_grouped, cosine_table, sine_table, -1.0)
            .astype(jnp.bfloat16)
            .reshape(group_rows, -1)
        )
        value_low = (
            grad_values.reshape(seq_count, LEN, key_count, -1, HD)
            .sum(axis=3)
            .astype(jnp.bfloat16)
            .reshape(group_rows, -1)
        )
        query_product = contract_rows(normed_all, query_low)
        key_product = contract_rows(normed_all, key_low)
        value_product = contract_rows(normed_all, value_low)
        if paired:
            key_back, value_back = (
                swapped(other_columns(key_product).astype(jnp.bfloat16), "tensor", 0).astype(
                    jnp.float32
                ),
                swapped(other_columns(value_product).astype(jnp.bfloat16), "tensor", 0).astype(
                    jnp.float32
                ),
            )
            key_product = own_columns(key_product) + key_back
            value_product = own_columns(value_product) + value_back
        collected[layer_index] = (query_product, key_product, value_product, out_product)
        if layer_index > 0:
            grad_part = contract_last(query_low, query_weight[layer_index])
            grad_part = (
                grad_part
                + contract_last(key_low, key_full[layer_index])
                + contract_last(value_low, value_full[layer_index])
            )
            grad_normed = lax.psum(grad_part.astype(jnp.bfloat16), "tensor").astype(jnp.float32)
            cotangent = cotangent + norm_back(
                wide_stream, inverse, grad_normed, norm_gains[layer_index]
            )
    query_stack = jnp.stack([collected[number][0] for number in range(layer_count)])
    key_stack = jnp.stack([collected[number][1] for number in range(layer_count)])
    value_stack = jnp.stack([collected[number][2] for number in range(layer_count)])
    out_stack = jnp.stack([collected[number][3] for number in range(layer_count)])
    query_stack, key_stack, value_stack, out_stack = (
        lax.psum_scatter(
            query_stack.astype(jnp.bfloat16), "dp", scatter_dimension=1, tiled=True
        ).astype(jnp.float32),
        lax.psum_scatter(
            key_stack.astype(jnp.bfloat16), "dp", scatter_dimension=1, tiled=True
        ).astype(jnp.float32),
        lax.psum_scatter(
            value_stack.astype(jnp.bfloat16), "dp", scatter_dimension=1, tiled=True
        ).astype(jnp.float32),
        lax.psum_scatter(
            out_stack.astype(jnp.bfloat16), "dp", scatter_dimension=2, tiled=True
        ).astype(jnp.float32),
    )
    return (query_stack, key_stack, value_stack, out_stack)


def solution(mesh):
    placed = (
        P(("dp", "tensor"), None),
        P(),
        P(),
        P(None, None, "tensor"),
        P(None, None, "tensor"),
        P(None, None, "tensor"),
        P(None, "tensor", None),
        P(None, "dp", "tensor"),
        P(None, "dp", "tensor"),
        P(None, "dp", "tensor"),
        P(None, "tensor", "dp"),
    )
    return jax.shard_map(
        body,
        mesh=mesh,
        in_specs=placed,
        out_specs=(
            P(None, "dp", "tensor"),
            P(None, "dp", "tensor"),
            P(None, "dp", "tensor"),
            P(None, "tensor", "dp"),
        ),
        check_vma=False,
    )
```

profile of v0, /device:TPU:0, one launch (start us, length us, event | category | flops | bytes accessed | tf_op | source)
XLA Modules:
  0.0 1128.5 jit_solution(12675295686108576268)
XLA Ops:
  10.6 5.8 slice_bitcast_fusion.8
  16.4 6.3 copy.15
  25.1 15.2 %all-gather.6.cloned.1.call-done = bf16[256,4096]{1,0:T(8,128)(2,1)} async-done(((bf16[32,4096]{1,0:T(8,128)(2,1)}), bf16[256,4096]{1,0:T(8,128)(2,1)}) %all-gather.6.cloned.1.call-update) | async-done | bytes 2097168 | tf_op jit(solution)/shard_map/all_gather | solution.py:189
  47.5 40.2 %all-gather.10.cloned.1.call-done = bf16[2,4096,128]{2,1,0:T(8,128)(2,1)} async-done(((bf16[2,1024,128]{2,1,0:T(8,128)(2,1)}), bf16[2,4096,128]{2,1,0:T(8,128)(2,1)}) %all-gather.10.cloned.1.call-update) | async-done | bytes 2097168 | tf_op jit(solution)/shard_map/all_gather | solution.py:176
  94.0 39.7 %all-gather.12.cloned.1.call-done = bf16[2,4096,128]{2,1,0:T(8,128)(2,1)} async-done(((bf16[2,1024,128]{2,1,0:T(8,128)(2,1)}), bf16[2,4096,128]{2,1,0:T(8,128)(2,1)}) %all-gather.12.cloned.1.call-update) | async-done | bytes 2097168 | tf_op jit(solution)/shard_map/all_gather | solution.py:177
  139.9 143.7 %all-gather.8.cloned.1.call-done = bf16[2,4096,512]{2,1,0:T(8,128)(2,1)} async-done(((bf16[2,1024,512]{2,1,0:T(8,128)(2,1)}), bf16[2,4096,512]{2,1,0:T(8,128)(2,1)}) %all-gather.8.cloned.1.call-update) | async-done | bytes 8388624 | tf_op jit(solution)/shard_map/all_gather | solution.py:175
  288.1 6.6 copy.18
  306.8 4.8 convolution_convert_fusion.4
  311.6 5.5 fusion.45
  317.1 115.8 %all-gather.14.cloned.1.call-done = bf16[2,512,4096]{2,1,0:T(8,128)(2,1)} async-done(((bf16[2,512,1024]{2,1,0:T(8,128)(2,1)}), bf16[2,512,4096]{2,1,0:T(8,128)(2,1)}) %all-gather.14.cloned.1.call-update) | async-done | bytes 8388624 | tf_op jit(solution)/shard_map/all_gather | solution.py:178
  432.9 6.1 fusion.6
  439.0 6.7 copy.28
  445.7 72.4 %all-reduce.9.cloned.1.call-done = (bf16[256,4096]{1,0:T(8,128)(2,1)}, bf16[256,4096]{1,0:T(8,128)(2,1)}) async-done(((bf16[256,4096]{1,0:T(8,128)(2,1)}, bf16[256,4096]{1,0:T(8,128)(2,1)}), (bf16[256,4096]{1,0:T(8,128)(2,1)}, bf16[256,4096]{1,0:T(8,128)(2,1)})) %all-reduce.9.cloned.1.call-update) | async-done | bytes 4194320 | tf_op jit(solution)/shard_map/psum | solution.py:245
  564.2 4.9 fusion.7
  569.9 61.3 %all-reduce.5.cloned.1.call-done = bf16[256,4096]{1,0:T(8,128)(2,1)} async-done(((bf16[256,4096]{1,0:T(8,128)(2,1)}), bf16[256,4096]{1,0:T(8,128)(2,1)}) %all-reduce.5.cloned.1.call-update) | async-done | bytes 2097168 | tf_op jit(solution)/shard_map/psum | solution.py:241
  631.2 4.8 fusion.95
  654.6 59.5 %all-reduce.7.cloned.1.call-done = bf16[256,4096]{1,0:T(8,128)(2,1)} async-done(((bf16[256,4096]{1,0:T(8,128)(2,1)}), bf16[256,4096]{1,0:T(8,128)(2,1)}) %all-reduce.7.cloned.1.call-update) | async-done | bytes 2097168 | tf_op jit(solution)/shard_map/psum | solution.py:305
  721.5 4.6 fusion.98
  754.7 7.6 pad_maximum_fusion
  763.8 5.2 fusion.5
  772.3 6.2 pad_maximum_fusion.1
  780.7 42.9 %reduce-scatter.9.cloned.1.call-done = bf16[2,1024,128]{2,1,0:T(8,128)(2,1)} async-done(((bf16[2,4096,128]{2,1,0:T(8,128)(2,1)}), bf16[2,1024,128]{2,1,0:T(8,128)(2,1)}) %reduce-scatter.9.cloned.1.call-update) | async-done | bytes 524304 | tf_op jit(solution)/shard_map/reduce_scatter | solution.py:320
  825.7 144.1 %reduce-scatter.5.cloned.1.call-done = bf16[2,1024,512]{2,1,0:T(8,128)(2,1)} async-done(((bf16[2,4096,512]{2,1,0:T(8,128)(2,1)}), bf16[2,1024,512]{2,1,0:T(8,128)(2,1)}) %reduce-scatter.5.cloned.1.call-update) | async-done | bytes 2097168 | tf_op jit(solution)/shard_map/reduce_scatter | solution.py:314
  974.0 143.3 %reduce-scatter.11.cloned.1.call-done = bf16[2,512,1024]{2,1,0:T(8,128)(2,1)} async-done(((bf16[2,512,4096]{2,1,0:T(8,128)(2,1)}), bf16[2,512,1024]{2,1,0:T(8,128)(2,1)}) %reduce-scatter.11.cloned.1.call-update) | async-done | bytes 2097168 | tf_op jit(solution)/shard_map/reduce_scatter | solution.py:323
  (237 shorter events, 159.8 us)
Async XLA Ops:
  7.2 33.2 %all-gather.6.cloned.1.call-start = ((), (), s32[]{:S(2)}) async-start(), calls=%async_computation.4 | async-start | bytes 2359296 | tf_op jit(solution)/shard_map/all_gather | solution.py:189
  7.9 79.8 %all-gather.10.cloned.1.call-start = ((), (), s32[]{:S(2)}) async-start(), calls=%async_computation.6 | async-start | bytes 2621440 | tf_op jit(solution)/shard_map/all_gather | solution.py:176
  8.6 125.1 %all-gather.12.cloned.1.call-start = ((), (), s32[]{:S(2)}) async-start(), calls=%async_computation.7 | async-start | bytes 2621440 | tf_op jit(solution)/shard_map/all_gather | solution.py:177
  9.4 274.2 %all-gather.8.cloned.1.call-start = ((), (), s32[]{:S(2)}) async-start(), calls=%async_computation.5 | async-start | bytes 10485760 | tf_op jit(solution)/shard_map/all_gather | solution.py:175
  10.0 422.9 %all-gather.14.cloned.1.call-start = ((), (), s32[]{:S(2)}) async-start(), calls=%async_computation.8 | async-start | bytes 10485760 | tf_op jit(solution)/shard_map/all_gather | solution.py:178
  10.5 507.6 %all-reduce.9.cloned.1.call-start = ((), (), s32[]{:S(2)}) async-start(), calls=%async_computation.15 | async-start | bytes 8388608 | tf_op jit(solution)/shard_map/psum | solution.py:245
  16.4 6.4 copy-start.56
  16.4 8.7 copy-start.42
  23.4 66.4 %copy-start.47 = (f32[64]{0:T(128)}, f32[64]{0:T(128)S(1)}, u32[]{:S(2)}) copy-start(f32[64]{0:T(128)S(1)} %multiply_exponential_fusion) | copy-start | bytes 772
  24.1 65.7 %copy-start.43 = (f32[256]{0:T(256)}, f32[256]{0:T(256)S(1)}, u32[]{:S(2)}) copy-start(f32[256]{0:T(256)S(1)} %iota_convert_fusion) | copy-start | bytes 3076
  44.7 250.0 %copy-start = (bf16[256,4096]{1,0:T(8,128)(2,1)}, bf16[256,4096]{1,0:T(8,128)(2,1)S(1)}, u32[]{:S(2)}) copy-start(bf16[256,4096]{1,0:T(8,128)(2,1)S(1)} %fusion.28) | copy-start | bytes 6291460
  298.7 7.3 copy-start.23
  298.8 7.3 copy-start.24
  439.0 192.2 %all-reduce.5.cloned.1.call-start = ((), (), s32[]{:S(2)}) async-start(), calls=%async_computation.9 | async-start | bytes 4194304 | tf_op jit(solution)/shard_map/psum | solution.py:241
  439.0 79.1 %copy-start.7 = (bf16[256,4096]{1,0:T(8,128)(2,1)S(1)}, bf16[256,4096]{1,0:T(8,128)(2,1)}, u32[]{:S(2)}) copy-start(bf16[256,4096]{1,0:T(8,128)(2,1)} %all-gather.6.cloned.1.call-done) | copy-start | bytes 6291460
  518.2 8.4 slice-start.2
  569.2 144.9 %all-reduce.7.cloned.1.call-start = ((), (), s32[]{:S(2)}) async-start(), calls=%async_computation.10 | async-start | bytes 4194304 | tf_op jit(solution)/shard_map/psum | solution.py:305
  569.9 61.3 %copy-start.53 = (f32[256]{0:T(256)}, f32[256]{0:T(256)S(1)}, u32[]{:S(2)}) copy-start(f32[256]{0:T(256)S(1)} %compare_convert_fusion) | copy-start | bytes 3076
  653.0 125.6 %reduce-scatter.7.cloned.1.call-start = ((), (), s32[]{:S(2)}) async-start(), calls=%async_computation.12 | async-start | bytes 2621440 | tf_op jit(solution)/shard_map/reduce_scatter | solution.py:317
  721.5 9.2 copy-start.46
  721.5 9.2 copy-start.50
  735.8 87.9 %reduce-scatter.9.cloned.1.call-start = ((), (), s32[]{:S(2)}) async-start(), calls=%async_computation.13 | async-start | bytes 2621440 | tf_op jit(solution)/shard_map/reduce_scatter | solution.py:320
  744.1 225.7 %reduce-scatter.5.cloned.1.call-start = ((), (), s32[]{:S(2)}) async-start(), calls=%async_computation.11 | async-start | bytes 10485760 | tf_op jit(solution)/shard_map/reduce_scatter | solution.py:314
  762.3 355.1 %reduce-scatter.11.cloned.1.call-start = ((), (), s32[]{:S(2)}) async-start(), calls=%async_computation.14 | async-start | bytes 10485760 | tf_op jit(solution)/shard_map/reduce_scatter | solution.py:323
  (49 other events, 161.9 us)
Sparse Core Ops, SparseCore 0:
  9.9 30.4 all-gather.5
  42.0 45.6 all-gather.9
  89.3 44.4 all-gather.11
  135.2 148.4 all-gather.7
  285.0 147.7 all-gather.13
  439.1 79.0 all-reduce.8
  569.3 61.8 all-reduce.4
  653.1 60.9 all-reduce.6
  735.9 42.6 reduce-scatter.6
  780.8 42.8 reduce-scatter.8
  826.0 143.7 reduce-scatter.4
  972.1 145.2 reduce-scatter.10
where the time goes:
time: 1140 us; the launch traced here: 1130 us
  waiting for transfers between devices  881 us (77%)
  matrix products  138 us (12%)
  other arithmetic  54.1 us (5%)
  local copies, waits for them, and re-layouts  38.4 us (3%)
  between operations  15.4 us (1%)
    reduce_scatter x1, waiting for transfers between devices, body(): lax.psum_scatter(query_stack.astype(jnp.bfloat16), 'dp', scatter_dimensio...  144 us
    all_gather x1, waiting for transfers between devices, body(): lax.all_gather(query_probe, 'dp', axis=1, tiled=True)  144 us
    reduce_scatter x1, waiting for transfers between devices, body(): lax.psum_scatter(out_stack.astype(jnp.bfloat16), 'dp', scatter_dimension=...  143 us
    all_gather x1, waiting for transfers between devices, body(): lax.all_gather(out_probe, 'dp', axis=2, tiled=True)  116 us
    psum x1, waiting for transfers between devices, body(): lax.psum(primal_part.astype(jnp.bfloat16), 'tensor').astype(jnp.float32)  72.4 us
    psum x1, waiting for transfers between devices, body(): lax.psum(tangent_part.astype(jnp.bfloat16), 'tensor').astype(jnp.float32)  61.3 us
    psum x1, waiting for transfers between devices, body(): lax.psum(grad_part.astype(jnp.bfloat16), 'tensor').astype(jnp.float32)  59.5 us
    dot_general x20, matrix products, matmul(): return jnp.dot(left_side, right_side, preferred_element_type=jnp.float32)  59.3 us
  transfers between devices with their start and end apart: 12, of which 12 were waited for; matrix products, arithmetic and copies ran while one was open for 11% of the time, Pallas kernels for 0%

commit v1 on v0

--- a/solution.py
+++ b/solution.py
@@ -242,7 +242,9 @@
         else:
             primal_part = matmul(blended, out_weight[layer_index])
             primal_sum, tangent_sum = (
-                lax.psum(primal_part.astype(jnp.bfloat16), "tensor").astype(jnp.float32),
+                jnp.sum(lax.all_gather(primal_part.astype(jnp.bfloat16), "tensor"), axis=0).astype(
+                    jnp.float32
+                ),
                 lax.psum(tangent_part.astype(jnp.bfloat16), "tensor").astype(jnp.float32),
             )
         stored.append((wide_stream, inverse, normed_all, queries, key_heads, value_heads, blended))

time: 1140 us -> 1210 us (1.061)
  waiting for transfers between devices: 881 us -> 937 us
  other arithmetic: 54.1 us -> 69.8 us
    all_gather x0 -> x1, waiting for transfers between devices: none -> 76.8 us  [body(): lax.all_gather(primal_part.astype(jnp.bfloat16), 'tensor')]
    psum x1 -> x0, waiting for transfers between devices: 72.4 us -> none  [body(): lax.psum(primal_part.astype(jnp.bfloat16), 'tensor').astype(jnp.float32)]
    psum x1 -> x2, waiting for transfers between devices: 61.3 us -> 114 us  [body(): lax.psum(tangent_part.astype(jnp.bfloat16), 'tensor').astype(jnp.float32)]
    reduce_scatter x1, waiting for transfers between devices: 42.9 us -> 0.02 us  [body(): lax.psum_scatter(value_stack.astype(jnp.bfloat16), 'dp', scatter_dimensio...]
    reduce_scatter x1, waiting for transfers between devices: 0.08 us -> 38.6 us  [body(): lax.psum_scatter(key_stack.astype(jnp.bfloat16), 'dp', scatter_dimension=...]
    all_gather x1, waiting for transfers between devices: 116 us -> 136 us  [body(): lax.all_gather(out_probe, 'dp', axis=2, tiled=True)]
    all_gather x1, waiting for transfers between devices: 39.7 us -> 23 us  [body(): lax.all_gather(value_probe, 'dp', axis=1, tiled=True)]
  transfers between devices with their start and end apart: 12 -> 13, of which waited for: 12 -> 12; matrix products, arithmetic and copies ran while one was open for 11% -> 12% of each run, Pallas kernels for 0% -> 0%
where the time goes in v1:
time: 1210 us; the launch traced here: 1200 us
  waiting for transfers between devices  937 us (77%)
  matrix products  138 us (11%)
  other arithmetic  69.8 us (6%)
  local copies, waits for them, and re-layouts  36.6 us (3%)
  between operations  15 us (1%)
    reduce_scatter x1, waiting for transfers between devices, body(): lax.psum_scatter(out_stack.astype(jnp.bfloat16), 'dp', scatter_dimension=...  144 us
    reduce_scatter x1, waiting for transfers between devices, body(): lax.psum_scatter(query_stack.astype(jnp.bfloat16), 'dp', scatter_dimensio...  144 us
    all_gather x1, waiting for transfers between devices, body(): lax.all_gather(query_probe, 'dp', axis=1, tiled=True)  142 us
    all_gather x1, waiting for transfers between devices, body(): lax.all_gather(out_probe, 'dp', axis=2, tiled=True)  136 us
    psum x2, waiting for transfers between devices, body(): lax.psum(tangent_part.astype(jnp.bfloat16), 'tensor').astype(jnp.float32)  114 us
    all_gather x1, waiting for transfers between devices, body(): lax.all_gather(primal_part.astype(jnp.bfloat16), 'tensor')  76.8 us
    psum x1, waiting for transfers between devices, body(): lax.psum(grad_part.astype(jnp.bfloat16), 'tensor').astype(jnp.float32)  59.3 us
    dot_general x20, matrix products, matmul(): return jnp.dot(left_side, right_side, preferred_element_type=jnp.float32)  54.6 us
  transfers between devices with their start and end apart: 13, of which 12 were waited for; matrix products, arithmetic and copies ran while one was open for 12% of the time, Pallas kernels for 0%

profile of v1, /device:TPU:0, one launch (start us, length us, event | category | flops | bytes accessed | tf_op | source)
XLA Modules:
  0.0 1196.5 jit_solution(4215428419927240356)
XLA Ops:
  10.6 5.8 slice_bitcast_fusion.8
  16.4 6.4 copy.15
  25.2 15.2 %all-gather.8.cloned.1.call-done = bf16[256,4096]{1,0:T(8,128)(2,1)} async-done(((bf16[32,4096]{1,0:T(8,128)(2,1)}), bf16[256,4096]{1,0:T(8,128)(2,1)}) %all-gather.8.cloned.1.call-update) | async-done | bytes 2097168 | tf_op jit(solution)/shard_map/all_gather | solution.py:189
  47.5 40.2 %all-gather.12.cloned.1.call-done = bf16[2,4096,128]{2,1,0:T(8,128)(2,1)} async-done(((bf16[2,1024,128]{2,1,0:T(8,128)(2,1)}), bf16[2,4096,128]{2,1,0:T(8,128)(2,1)}) %all-gather.12.cloned.1.call-update) | async-done | bytes 2097168 | tf_op jit(solution)/shard_map/all_gather | solution.py:176
  95.4 142.3 %all-gather.10.cloned.1.call-done = bf16[2,4096,512]{2,1,0:T(8,128)(2,1)} async-done(((bf16[2,1024,512]{2,1,0:T(8,128)(2,1)}), bf16[2,4096,512]{2,1,0:T(8,128)(2,1)}) %all-gather.10.cloned.1.call-update) | async-done | bytes 8388624 | tf_op jit(solution)/shard_map/all_gather | solution.py:175
  242.2 6.4 copy.18
  260.0 23.0 %all-gather.14.cloned.1.call-done = bf16[2,4096,128]{2,1,0:T(8,128)(2,1)} async-done(((bf16[2,1024,128]{2,1,0:T(8,128)(2,1)}), bf16[2,4096,128]{2,1,0:T(8,128)(2,1)}) %all-gather.14.cloned.1.call-update) | async-done | bytes 2097168 | tf_op jit(solution)/shard_map/all_gather | solution.py:177
  290.7 6.1 fusion.45
  296.8 136.1 %all-gather.16.cloned.1.call-done = bf16[2,512,4096]{2,1,0:T(8,128)(2,1)} async-done(((bf16[2,512,1024]{2,1,0:T(8,128)(2,1)}), bf16[2,512,4096]{2,1,0:T(8,128)(2,1)}) %all-gather.16.cloned.1.call-update) | async-done | bytes 8388624 | tf_op jit(solution)/shard_map/all_gather | solution.py:178
  432.9 6.1 fusion.6
  439.0 6.7 copy.28
  445.8 76.8 %all-gather.18.cloned.1.call-done = bf16[2048,4096]{1,0:T(8,128)(2,1)} async-done(((bf16[256,4096]{1,0:T(8,128)(2,1)}), bf16[2048,4096]{1,0:T(8,128)(2,1)}) %all-gather.18.cloned.1.call-update) | async-done | bytes 16777232 | tf_op jit(solution)/shard_map/all_gather | solution.py:245
  522.5 10.8 reduce_sum.141
  533.4 54.2 %all-reduce.4.cloned.1.call-done = bf16[256,4096]{1,0:T(8,128)(2,1)} async-done(((bf16[256,4096]{1,0:T(8,128)(2,1)}), bf16[256,4096]{1,0:T(8,128)(2,1)}) %all-reduce.4.cloned.1.call-update) | async-done | bytes 2097168 | tf_op jit(solution)/shard_map/psum | solution.py:248
  633.8 4.9 fusion.7
  639.5 60.3 %all-reduce.6.cloned.1.call-done = bf16[256,4096]{1,0:T(8,128)(2,1)} async-done(((bf16[256,4096]{1,0:T(8,128)(2,1)}), bf16[256,4096]{1,0:T(8,128)(2,1)}) %all-reduce.6.cloned.1.call-update) | async-done | bytes 2097168 | tf_op jit(solution)/shard_map/psum | solution.py:241
  725.1 59.3 %all-reduce.8.cloned.1.call-done = bf16[256,4096]{1,0:T(8,128)(2,1)} async-done(((bf16[256,4096]{1,0:T(8,128)(2,1)}), bf16[256,4096]{1,0:T(8,128)(2,1)}) %all-reduce.8.cloned.1.call-update) | async-done | bytes 2097168 | tf_op jit(solution)/shard_map/psum | solution.py:307
  791.8 5.3 fusion.98
  816.5 5.8 fusion.5
  825.6 7.6 pad_maximum_fusion.1
  843.6 7.5 pad_maximum_fusion
  853.3 38.6 %reduce-scatter.7.cloned.1.call-done = bf16[2,1024,128]{2,1,0:T(8,128)(2,1)} async-done(((bf16[2,4096,128]{2,1,0:T(8,128)(2,1)}), bf16[2,1024,128]{2,1,0:T(8,128)(2,1)}) %reduce-scatter.7.cloned.1.call-update) | async-done | bytes 524304 | tf_op jit(solution)/shard_map/reduce_scatter | solution.py:319
  893.9 144.0 %reduce-scatter.11.cloned.1.call-done = bf16[2,512,1024]{2,1,0:T(8,128)(2,1)} async-done(((bf16[2,512,4096]{2,1,0:T(8,128)(2,1)}), bf16[2,512,1024]{2,1,0:T(8,128)(2,1)}) %reduce-scatter.11.cloned.1.call-update) | async-done | bytes 2097168 | tf_op jit(solution)/shard_map/reduce_scatter | solution.py:325
  1042.0 143.6 %reduce-scatter.5.cloned.1.call-done = bf16[2,1024,512]{2,1,0:T(8,128)(2,1)} async-done(((bf16[2,4096,512]{2,1,0:T(8,128)(2,1)}), bf16[2,1024,512]{2,1,0:T(8,128)(2,1)}) %reduce-scatter.5.cloned.1.call-update) | async-done | bytes 2097168 | tf_op jit(solution)/shard_map/reduce_scatter | solution.py:316
  (239 shorter events, 168.5 us)
Async XLA Ops:
  7.2 33.2 %all-gather.8.cloned.1.call-start = ((), (), s32[]{:S(2)}) async-start(), calls=%async_computation.4 | async-start | bytes 2359296 | tf_op jit(solution)/shard_map/all_gather | solution.py:189
  7.9 79.8 %all-gather.12.cloned.1.call-start = ((), (), s32[]{:S(2)}) async-start(), calls=%async_computation.6 | async-start | bytes 2621440 | tf_op jit(solution)/shard_map/all_gather | solution.py:176
  8.6 229.0 %all-gather.10.cloned.1.call-start = ((), (), s32[]{:S(2)}) async-start(), calls=%async_computation.5 | async-start | bytes 10485760 | tf_op jit(solution)/shard_map/all_gather | solution.py:175
  9.4 273.6 %all-gather.14.cloned.1.call-start = ((), (), s32[]{:S(2)}) async-start(), calls=%async_computation.7 | async-start | bytes 2621440 | tf_op jit(solution)/shard_map/all_gather | solution.py:177
  10.0 422.9 %all-gather.16.cloned.1.call-start = ((), (), s32[]{:S(2)}) async-start(), calls=%async_computation.8 | async-start | bytes 10485760 | tf_op jit(solution)/shard_map/all_gather | solution.py:178
  10.5 512.0 %all-gather.18.cloned.1.call-start = ((), (), s32[]{:S(2)}) async-start(), calls=%async_computation.16 | async-start | bytes 18874368 | tf_op jit(solution)/shard_map/all_gather | solution.py:245
  23.5 66.4 %copy-start.47 = (f32[64]{0:T(128)}, f32[64]{0:T(128)S(1)}, u32[]{:S(2)}) copy-start(f32[64]{0:T(128)S(1)} %multiply_exponential_fusion) | copy-start | bytes 772
  24.1 65.8 %copy-start.44 = (f32[256]{0:T(256)}, f32[256]{0:T(256)S(1)}, u32[]{:S(2)}) copy-start(f32[256]{0:T(256)S(1)} %iota_convert_fusion) | copy-start | bytes 3076
  44.7 238.3 %copy-start = (bf16[256,4096]{1,0:T(8,128)(2,1)}, bf16[256,4096]{1,0:T(8,128)(2,1)S(1)}, u32[]{:S(2)}) copy-start(bf16[256,4096]{1,0:T(8,128)(2,1)S(1)} %fusion.28) | copy-start | bytes 6291460
  259.6 25.9 %copy-start.20 = (bf16[256,4,64]{0,2,1:T(8,128)(2,1)S(1)}, bf16[256,4,64]{0,2,1:T(8,128)(2,1)}, u32[]{:S(2)}) copy-start(bf16[256,4,64]{0,2,1:T(8,128)(2,1)} %get-tuple-element.106) | copy-start | bytes 393220
  259.6 25.9 %copy-start.21 = (bf16[256,4,64]{0,2,1:T(8,128)(2,1)S(1)}, bf16[256,4,64]{0,2,1:T(8,128)(2,1)}, u32[]{:S(2)}) copy-start(bf16[256,4,64]{0,2,1:T(8,128)(2,1)} %get-tuple-element.116) | copy-start | bytes 393220
  259.6 25.9 %copy-start.41 = (pred[256,256]{0,1:T(8,128)(4,1)S(1)}, pred[256,256]{0,1:T(8,128)(4,1)}, u32[]{:S(2)}) copy-start(pred[256,256]{0,1:T(8,128)(4,1)} %fusion.161) | copy-start | bytes 196612
  259.6 327.9 %all-reduce.4.cloned.1.call-start = ((), (), s32[]{:S(2)}) async-start(), calls=%async_computation.9 | async-start | bytes 4194304 | tf_op jit(solution)/shard_map/psum | solution.py:248
  439.0 260.8 %all-reduce.6.cloned.1.call-start = ((), (), s32[]{:S(2)}) async-start(), calls=%async_computation.10 | async-start | bytes 4194304 | tf_op jit(solution)/shard_map/psum | solution.py:241
  522.5 65.0 %copy-start.6 = (bf16[256,4096]{1,0:T(8,128)(2,1)S(1)}, bf16[256,4096]{1,0:T(8,128)(2,1)}, u32[]{:S(2)}) copy-start(bf16[256,4096]{1,0:T(8,128)(2,1)} %all-gather.8.cloned.1.call-done) | copy-start | bytes 6291460
  638.8 145.7 %all-reduce.8.cloned.1.call-start = ((), (), s32[]{:S(2)}) async-start(), calls=%async_computation.11 | async-start | bytes 4194304 | tf_op jit(solution)/shard_map/psum | solution.py:307
  639.4 65.1 %copy-start.52 = (f32[256]{0:T(256)}, f32[256]{0:T(256)S(1)}, u32[]{:S(2)}) copy-start(f32[256]{0:T(256)S(1)} %compare_convert_fusion) | copy-start | bytes 3076
  639.4 65.8 %copy-start.23 = (bf16[256,4,64]{0,2,1:T(8,128)(2,1)S(1)}, bf16[256,4,64]{0,2,1:T(8,128)(2,1)}, u32[]{:S(2)}) copy-start(bf16[256,4,64]{0,2,1:T(8,128)(2,1)} %copy-done.22) | copy-start | bytes 393220
  639.4 65.8 %copy-start.25 = (bf16[256,4,64]{0,2,1:T(8,128)(2,1)S(1)}, bf16[256,4,64]{0,2,1:T(8,128)(2,1)}, u32[]{:S(2)}) copy-start(bf16[256,4,64]{0,2,1:T(8,128)(2,1)} %copy-done.24) | copy-start | bytes 393220
  639.5 65.8 %copy-start.36 = (bf16[256,128]{0,1:T(8,128)(2,1)S(1)}, bf16[256,128]{0,1:T(8,128)(2,1)}, u32[]{:S(2)}) copy-start(bf16[256,128]{0,1:T(8,128)(2,1)} %copy-done.35) | copy-start | bytes 196612
  723.5 127.7 %reduce-scatter.9.cloned.1.call-start = ((), (), s32[]{:S(2)}) async-start(), calls=%async_computation.14 | async-start | bytes 2621440 | tf_op jit(solution)/shard_map/reduce_scatter | solution.py:322
  803.8 88.0 %reduce-scatter.7.cloned.1.call-start = ((), (), s32[]{:S(2)}) async-start(), calls=%async_computation.13 | async-start | bytes 2621440 | tf_op jit(solution)/shard_map/reduce_scatter | solution.py:319
  816.4 221.5 %reduce-scatter.11.cloned.1.call-start = ((), (), s32[]{:S(2)}) async-start(), calls=%async_computation.15 | async-start | bytes 10485760 | tf_op jit(solution)/shard_map/reduce_scatter | solution.py:325
  833.2 352.3 %reduce-scatter.5.cloned.1.call-start = ((), (), s32[]{:S(2)}) async-start(), calls=%async_computation.12 | async-start | bytes 10485760 | tf_op jit(solution)/shard_map/reduce_scatter | solution.py:316
  (49 other events, 280.0 us)
Sparse Core Ops, SparseCore 0:
  9.9 30.4 all-gather.7
  42.0 45.6 all-gather.11
  89.3 148.3 all-gather.9
  239.1 43.8 all-gather.13
  284.4 148.4 all-gather.15
  434.6 87.9 all-gather.17
  525.8 61.7 all-reduce.3
  638.9 60.8 all-reduce.5
  723.6 60.8 all-reduce.7
  803.9 42.6 reduce-scatter.8
  849.0 42.8 reduce-scatter.6
  894.0 143.7 reduce-scatter.10
  1040.2 145.2 reduce-scatter.4
